TPU v7x, 128 devices: a whole 4x4x4 slice. The times are simulated.
128 devices in a mesh: seq: 8 (over y_lo, x), exp: 16 (over y_hi, z, core).
Axes of the slice: x: 4, y: 4 (y_hi: 2, y_lo: 2; y = y_hi * 2 + y_lo), z: 4, core: 2. Of those that a mesh axis runs over, the one named last changes fastest.
Arguments:
- gates: float32 [16384, 2], P(('seq', 'exp')), may hold values from 0.1 to 0.9
- expert_ids: int32 [16384, 2], P(('seq', 'exp')), may hold values from 0 to 15, all different within a row; in each aligned block of 128 rows (0 to 127, 128 to 255, ...) at most 16 rows name the same one
- saved_pre: bfloat16 [16, 2048, 2, 7168], P('exp', None, None, 'seq'), may hold values from -6 to 6
- w_down: bfloat16 [16, 7168, 4096], P('exp', 'seq'), may hold values from -0.0625 to 0.0625
- residual_grad: bfloat16 [16384, 4096], P(('seq', 'exp')), may hold values from -6 to 6
- in_weight: bfloat16 [4096, 4096], P('seq', 'exp'), may hold values from -0.09375 to 0.09375
- ssm_in: bfloat16 [16384, 4096], P('seq', 'exp'), may hold values from -0.59765625 to 0.59765625
- b_proj: bfloat16 [16384, 128], P('seq'), may hold values from -0.546875 to 0.546875
- c_proj: bfloat16 [16384, 128], P('seq'), may hold values from -0.546875 to 0.546875
- step_sizes: float32 [64, 16384], P('exp', 'seq'), may hold values from 0.05 to 4590.52
- a_log: float32 [64], P('exp'), may hold values from -12 to 0
- skip_gain: float32 [64], P('exp'), may hold values from 0.5 to 1.5
- ssm_grad: bfloat16 [16384, 4096], P('seq', 'exp'), may hold values from -6 to 6
Outputs:
- pre_grads: bfloat16 [16, 2048, 2, 7168], P('exp', None, None, 'seq')
- route_grads: float32 [16384, 2], P(('seq', 'exp'))
- b_grads: float32 [16384, 128], P(('seq', 'exp'))
- c_grads: float32 [16384, 128], P(('seq', 'exp'))
- step_grads: float32 [64, 16384], P('exp', 'seq')
Inputs may be any that keep to these rules, and one draw needn't show every extreme that they name: `expert_ids`: in each aligned block of 128 rows every expert is named by exactly 16 entries, and a row names 2 different experts.
All inputs are finite; a program needn't handle non-finite values.
Results may differ from a plain program's by a relative error of at most 0.019.
Values may be sent and summed in bfloat16 or wider, within the bound.
A program may use at most 192 MiB of HBM per device.

v0:
```python
import jax
import jax.numpy as jnp
from jax import lax
from jax.sharding import Mesh
from jax.sharding import PartitionSpec as P

TOPK = 2
HDIM = 64
SPAN = 256
EXP = ("exp_0", "exp_1", "exp_2")
SEQ_EXP = ("seq", "exp_0", "exp_1", "exp_2")


def in_blocks(array, dim, count):
    shape = array.shape
    tiles = array.reshape(*shape[:dim], count, shape[dim] // count, *shape[dim + 1 :])
    return jnp.moveaxis(tiles, dim, 0)


def summed_on_arrival(array, axis, dim):
    count = lax.axis_size(axis)
    tiles = lax.all_to_all(in_blocks(array, dim, count), axis, 0, 0, tiled=True)
    return jnp.sum(tiles, axis=0)


def copy_for_each(array, axis):
    copies = jnp.broadcast_to(array, (lax.axis_size(axis), *array.shape))
    return lax.all_to_all(copies, axis, split_axis=0, concat_axis=0, tiled=True)


def folded_in_pairs(pieces, combine):
    while len(jax.tree.leaves(pieces)[0]) > 1:
        pieces = jax.vmap(combine)(
            *(jax.tree.map(lambda part: part[side::2], pieces) for side in (0, 1))
        )
    return jax.tree.map(lambda part: part[0], pieces)


def carried_in(array, axis, combine, identity, reverse):
    count, here = (lax.axis_size(axis), lax.axis_index(axis))
    passed = jnp.arange(count) > here if reverse else jnp.arange(count) < here

    def kept(part, zero, own):
        part = jnp.where(
            passed.reshape(-1, *(1 for _ in own.shape)), part, jnp.asarray(zero, own.dtype)
        )
        return part[::-1] if reverse else part

    pieces = jax.tree.map(lambda part: copy_for_each(part, axis), array)
    return folded_in_pairs(jax.tree.map(kept, pieces, identity, array), combine)


def in_one_piece(arrays, axis, dim, along):
    ends, at = ([], 0)
    for a in arrays[:-1]:
        at += a.shape[along]
        ends.append(at)
    both = jnp.concatenate(arrays, axis=along)
    return tuple(
        jnp.split(lax.psum_scatter(both, axis, scatter_dimension=dim, tiled=True), ends, axis=along)
    )


def laid_out(tiles, dim):
    tiles = jnp.moveaxis(tiles, 0, dim)
    shape = tiles.shape
    return tiles.reshape(*shape[:dim], shape[dim] * shape[dim + 1], *shape[dim + 2 :])


def gathered_copies(array, axis, dim):
    tiles = copy_for_each(array, axis)
    return laid_out(tiles, dim)


def summed_rows(array, chips, core, dim):
    sizes = (lax.axis_size(chips), lax.axis_size(core))
    tiles = in_blocks(array, dim, sizes[0] * sizes[1])
    inside = tiles.shape[1:]
    tiles = tiles.reshape(*sizes, *inside).swapaxes(0, 1).reshape(-1, *inside)
    tiles = lax.psum_scatter(tiles, core, scatter_dimension=0, tiled=True)
    return lax.psum_scatter(tiles, chips, scatter_dimension=0, tiled=True)[0]


def span_scan(heads_input, b_values, c_values, log_decay, skip_values, start_state):
    head_count, length, head_size = heads_input.shape
    state_size = b_values.shape[1]
    blocks = length // SPAN
    x_spans = heads_input.reshape(head_count, blocks, SPAN, head_size).transpose(1, 0, 2, 3)
    b_spans = b_values.reshape(blocks, SPAN, state_size)
    c_spans = c_values.reshape(blocks, SPAN, state_size)
    g_spans = log_decay.reshape(head_count, blocks, SPAN).transpose(1, 0, 2)
    lower_mask = jnp.tril(jnp.ones((SPAN, SPAN), jnp.bool_))

    def advance(carried_state, inputs):
        x_block, b_block, c_block, g_block = inputs
        cumulative = jnp.cumsum(g_block, axis=1)
        spread = cumulative[:, :, None] - cumulative[:, None, :]
        weights = jnp.where(lower_mask, jnp.exp(-jnp.where(lower_mask, spread, 0.0)), 0.0)
        scores = jnp.dot(c_block, b_block.T)
        within = jnp.einsum("hij,ij,hjp->hip", weights, scores, x_block)
        carried = jnp.einsum("hi,in,hpn->hip", jnp.exp(-cumulative), c_block, carried_state)
        tail_decay = jnp.exp(cumulative - cumulative[:, -1:])
        fresh_state = jnp.einsum("hj,hjp,jn->hpn", tail_decay, x_block, b_block)
        next_state = jnp.exp(-cumulative[:, -1])[:, None, None] * carried_state + fresh_state
        return (next_state, within + carried)

    final_state, outputs = lax.scan(advance, start_state, (x_spans, b_spans, c_spans, g_spans))
    output = outputs.transpose(1, 0, 2, 3).reshape(head_count, length, head_size)
    return (output + skip_values[:, None, None] * heads_input, final_state)


def swiglu_grads(upstream, gate_values, saved_rows):
    gate_pre = saved_rows[:, 0, :].astype(jnp.float32)
    up_pre = saved_rows[:, 1, :].astype(jnp.float32)
    sigmoid_gate = jax.nn.sigmoid(gate_pre)
    activated = gate_pre * sigmoid_gate
    route_part = jnp.sum(activated * up_pre * upstream, axis=1)
    hidden_grad = gate_values[:, None] * upstream
    gate_grad = hidden_grad * up_pre * sigmoid_gate * (1.0 + gate_pre * (1.0 - sigmoid_gate))
    up_grad = hidden_grad * activated
    return (jnp.stack([gate_grad, up_grad], axis=1).astype(jnp.bfloat16), route_part)


def chain_join(earlier, latter):
    return (earlier[0] * latter[0], latter[0][:, None, None] * earlier[1] + latter[1])


def moe_part(moe_grad, gates, expert_ids, saved_pre, w_down):
    tokens_here = moe_grad.shape[0]
    expert_count = lax.axis_size(EXP)
    group_count = lax.axis_size("seq")
    capacity = TOPK * tokens_here // expert_count
    flat_ids = expert_ids.reshape(-1)
    onehot = (flat_ids[:, None] == jnp.arange(expert_count, dtype=jnp.int32)[None, :]).astype(
        jnp.int32
    )
    running = jnp.cumsum(onehot, axis=0)
    position = jnp.sum(onehot * running, axis=1) - 1
    target = flat_ids * capacity + position
    selector = target[:, None] == jnp.arange(expert_count * capacity, dtype=jnp.int32)[None, :]
    repeated = jnp.repeat(moe_grad, TOPK, axis=0)
    outgoing = lax.dot_general(
        selector.astype(jnp.bfloat16),
        repeated,
        (((0,), (0,)), ((), ())),
        preferred_element_type=jnp.float32,
    )
    outgoing = outgoing.astype(jnp.bfloat16).reshape(expert_count, capacity, moe_grad.shape[1])
    outgoing_gates = lax.dot_general(
        selector.astype(jnp.float32), gates.reshape(-1), (((0,), (0,)), ((), ()))
    )
    outgoing_gates = outgoing_gates.reshape(expert_count, capacity)
    weight = w_down[0]
    saved_rows = saved_pre[0]
    arrived = (
        lax.all_to_all(outgoing, EXP, split_axis=0, concat_axis=0, tiled=True),
        lax.all_to_all(
            outgoing_gates.astype(jnp.bfloat16), EXP, split_axis=0, concat_axis=0, tiled=True
        ).astype(outgoing_gates.dtype),
    )
    gathered, arrived_gates = (
        lax.all_gather(arrived[0], "seq", axis=0, tiled=True),
        lax.all_gather(arrived[1].astype(jnp.bfloat16), "seq", axis=0, tiled=True).astype(
            jnp.float32
        ),
    )
    upstream = lax.dot_general(
        gathered,
        weight,
        (((gathered.ndim - 1,), (1,)), ((), ())),
        preferred_element_type=jnp.float32,
    )
    slot_count = upstream.shape[0] * upstream.shape[1]
    pre_grad, route_part = swiglu_grads(
        upstream.reshape(slot_count, -1), arrived_gates.reshape(-1), saved_rows
    )
    route_part = route_part.reshape(group_count * expert_count, capacity)
    partial_value = summed_on_arrival(route_part, "seq", 0)
    totals = lax.all_to_all(partial_value, EXP, split_axis=0, concat_axis=0, tiled=True)
    route_grads = totals.reshape(-1)[target].reshape(tokens_here, TOPK)
    return (pre_grad[None], route_grads)


def ssm_part(ssm_in, b_proj, c_proj, step_sizes, a_log, skip_gain, ssm_grad):
    length, columns = ssm_in.shape
    head_count = columns // HDIM
    heads_input = ssm_in.astype(jnp.float32).reshape(length, head_count, HDIM).transpose(1, 0, 2)
    grads_heads = ssm_grad.astype(jnp.float32).reshape(length, head_count, HDIM).transpose(1, 0, 2)
    b_values = b_proj.astype(jnp.float32)
    c_values = c_proj.astype(jnp.float32)
    decay_rates = jnp.exp(a_log)
    log_decay = step_sizes * decay_rates[:, None]
    cumulative = jnp.cumsum(log_decay, axis=1)
    chain_total = cumulative[:, -1]
    shard_decay = jnp.exp(-chain_total)
    end_state = jnp.einsum(
        "ht,htp,tn->hpn", jnp.exp(cumulative - chain_total[:, None]), heads_input, b_values
    )
    entry_grad = jnp.einsum("ht,htp,tn->hpn", jnp.exp(-cumulative), grads_heads, c_values)
    identity = (jnp.ones_like(shard_decay), jnp.zeros_like(end_state))
    entry_state = carried_in((shard_decay, end_state), "seq", chain_join, identity, False)[1]
    exit_grad = carried_in((shard_decay, entry_grad), "seq", chain_join, identity, True)[1]

    def local_forward(inputs, b_local, c_local, log_rates):
        return span_scan(inputs, b_local, c_local, log_rates, skip_gain, entry_state)

    unused, pullback = jax.vjp(local_forward, heads_input, b_values, c_values, log_decay)
    input_heads, b_grad, c_grad, decay_grad = pullback((grads_heads, exit_grad))
    step_grads = decay_grad * decay_rates[:, None]
    x_grad = input_heads.transpose(1, 0, 2).reshape(length, columns).astype(jnp.bfloat16)
    b_grads, c_grads = in_one_piece((b_grad, c_grad), EXP, 0, 1)
    return (x_grad, b_grads, c_grads, step_grads)


def per_device(
    gates,
    expert_ids,
    saved_pre,
    w_down,
    residual_grad,
    in_weight,
    ssm_in,
    b_proj,
    c_proj,
    step_sizes,
    a_log,
    skip_gain,
    ssm_grad,
):
    x_grad, b_grads, c_grads, step_grads = ssm_part(
        ssm_in, b_proj, c_proj, step_sizes, a_log, skip_gain, ssm_grad
    )
    whole_weight = gathered_copies(in_weight, "seq", 0)
    summed = summed_rows(
        lax.dot_general(
            x_grad, whole_weight, (((1,), (1,)), ((), ())), preferred_element_type=jnp.float32
        ).astype(jnp.bfloat16),
        ("exp_0", "exp_1"),
        "exp_2",
        0,
    ).astype(jnp.float32)
    moe_grad = (residual_grad.astype(jnp.float32) + summed).astype(jnp.bfloat16)
    pre_grads, route_grads = moe_part(moe_grad, gates, expert_ids, saved_pre, w_down)
    return (pre_grads, route_grads, b_grads, c_grads, step_grads)


def solution(mesh):
    split = Mesh(
        mesh.devices.reshape(mesh.shape["seq"], 2, 4, 2), ("seq", "exp_0", "exp_1", "exp_2")
    )
    in_specs = (
        P(SEQ_EXP, None),
        P(SEQ_EXP, None),
        P(EXP, None, None, "seq"),
        P(EXP, "seq", None),
        P(SEQ_EXP, None),
        P("seq", EXP),
        P("seq", EXP),
        P("seq", None),
        P("seq", None),
        P(EXP, "seq"),
        P(EXP),
        P(EXP),
        P("seq", EXP),
    )
    out_specs = (
        P(EXP, None, None, "seq"),
        P(SEQ_EXP, None),
        P(SEQ_EXP, None),
        P(SEQ_EXP, None),
        P(EXP, "seq"),
    )
    return jax.shard_map(
        per_device, mesh=split, in_specs=in_specs, out_specs=out_specs, check_vma=False
    )
```

profile of v0, /device:TPU:1, one launch (start us, length us, event | category | flops | bytes accessed | tf_op | source)
XLA Modules:
  0.0 862.5 jit_solution(5964369956891193884)
XLA Ops:
  11.9 5.9 all-to-all-start.1
  28.1 5.1 all-to-all-start.2
  36.0 13.2 %all-to-all-done.2 = f32[8,4,64,128]{3,2,1,0:T(8,128)} async-done(((f32[8,4,64,128]{3,2,1,0:T(8,128)}), f32[8,4,64,128]{3,2,1,0:T(8,128)}, u32[]{:S(2)}, u32[]{:S(2)}) %all-to-all-start.2) | async-done | bytes 1048608 | tf_op jit(solution)/shard_map/all_to_all | solution.py:28
  58.8 11.0 %all-to-all-done.3 = f32[8,4,64,128]{3,2,1,0:T(8,128)S(1)} async-done(((f32[8,4,64,128]{3,2,1,0:T(8,128)}), f32[8,4,64,128]{3,2,1,0:T(8,128)S(1)}, u32[]{:S(2)}, u32[]{:S(2)}) %all-to-all-start.3) | async-done | bytes 1048608 | tf_op jit(solution)/shard_map/all_to_all | solution.py:28
  78.3 117.4 %while.65 = (s32[]{:T(128)}, f32[4,64,128]{2,1,0:T(8,128)S(1)}, f32[8,4,256,256]{3,2,1,0:T(8,128)}, bf16[8,128,256]{1,2,0:T(8,128)(2,1)}, f32[8,256,256]{2,1,0:T...) while((s32[]{:T(128)}, f32[4,64,128]{2,1,0:T(8,128)S(1)}, ...), condition=%wide.region_8.9_spmd.clone.clone.clone, body=%wide.region_5.8_spmd.clone.clone.sunk.clone | while | flops 53022744 | bytes 6271773 | solution.py:107
  199.7 193.4 %while.66 = (s32[]{:T(128)}, f32[4,64,128]{2,1,0:T(8,128)S(1)}, f32[8,4,256,64]{2,3,1,0:T(8,128)}, f32[8,256,128]{2,1,0:T(8,128)}, f32[8,256,128]{2,1,0:T(8,128)...) while((s32[]{:T(128)}, f32[4,64,128]{2,1,0:T(8,128)S(1)}, ...), condition=%wide.region_16.17_spmd.clone.clone.clone, body=%wide.region_9.16_spmd.clone.clone.sunk.clone | while | flops 170925072 | bytes 11393397 | solution.py:107
  213.7 5.0 reduce-window.78
  237.9 5.0 reduce-window.78
  262.1 5.0 reduce-window.78
  310.4 5.0 reduce-window.78
  334.6 5.0 reduce-window.78
  358.8 5.0 reduce-window.78
  395.5 9.7 %convolution_convert_fusion = bf16[2048,4096]{1,0:T(8,128)(2,1)} fusion(bf16[2048,256]{0,1:T(8,128)(2,1)S(1)} %bitcast.518, bf16[4096,256]{1,0:T(8,128)(2,1)} %bitcast.27), kind=kOutput, calls=%fused_computation.113 | convolution fusion | flops 4303355904 | bytes 19922944 | tf_op jit(solution)/shard_map/dot_general | solution.py:235
  405.2 14.0 %copy.201 = bf16[2,8,128,4096]{3,2,1,0:T(8,128)(2,1)} copy(bf16[2,8,128,4096]{3,2,0,1:T(8,128)(2,1)} %bitcast.505) | data formatting | bytes 33554432 | tf_op jit(solution)/shard_map/transpose | solution.py:79
  419.3 30.6 %reduce-scatter.4.cloned.1.call-done = bf16[8,128,4096]{2,1,0:T(8,128)(2,1)} async-done(((bf16[16,128,4096]{2,1,0:T(8,128)(2,1)}), bf16[8,128,4096]{2,1,0:T(8,128)(2,1)}) %reduce-scatter.4.cloned.1.call-update) | async-done | bytes 8388624 | tf_op jit(solution)/shard_map/reduce_scatter | solution.py:80
  451.9 116.8 %reduce-scatter.6.cloned.1.call-done = bf16[1,128,4096]{2,1,0:T(8,128)(2,1)} async-done(((bf16[8,128,4096]{2,1,0:T(8,128)(2,1)}), bf16[1,128,4096]{2,1,0:T(8,128)(2,1)}) %reduce-scatter.6.cloned.1.call-update) | async-done | bytes 1048592 | tf_op jit(solution)/shard_map/reduce_scatter | solution.py:81
  577.0 32.7 %all_to_all.56 = bf16[16,16,4096]{2,1,0:T(8,128)(2,1)} all-to-all(bf16[16,16,4096]{2,1,0:T(8,128)(2,1)S(1)} %bitcast.514), channel_id=1, replica_groups=mesh['seq'=8,'exp_0'=2,'exp_1'=4,'exp_2'=2] {'exp_0','exp_1','exp_2'}, dimensions={0} | all-to-all | bytes 4194304 | tf_op jit(solution)/shard_map/all_to_all | solution.py:156
  616.0 18.8 %copy.202 = bf16[1,2048,2,896]{1,3,2,0:T(8,128)(2,1)} copy(bf16[1,2048,2,896]{3,2,1,0:T(2,128)(2,1)} %param.19) | data formatting | bytes 14680064 | tf_op args[2]
  634.8 25.3 %all-gather = bf16[128,1,16]{2,0,1:T(8,128)(2,1)S(1)} all-gather(bf16[16,1,16]{2,0,1:T(8,128)(2,1)S(1)} %copy.186), channel_id=2, replica_groups=mesh['seq'=8,'exp_0'=2,'exp_1'=4,'exp_2'=2] {'seq'}, dimensions={0}, use_global_device_ids=true | all-gather | bytes 4608 | tf_op jit(solution)/shard_map/all_gather | solution.py:163
  662.5 115.7 %all-gather.3.cloned.1.call-done = bf16[128,16,4096]{2,1,0:T(8,128)(2,1)} async-done(((bf16[16,16,4096]{2,1,0:T(8,128)(2,1)}), bf16[128,16,4096]{2,1,0:T(8,128)(2,1)}) %all-gather.3.cloned.1.call-update) | async-done | bytes 16777232 | tf_op jit(solution)/shard_map/all_gather | solution.py:162
  778.2 28.0 %fusion.80 = (bf16[1,2048,1,896]{1,3,2,0:T(8,128)(2,1)}, bf16[1,2048,1,896]{1,3,2,0:T(8,128)(2,1)}, f32[2048]{0:T(1024)S(1)}) fusion(f32[2048]{0:T(1024)S(1)} %reshape.592, bf16[2048,2,896]{0,2,1:T(8,128)(2,1)} %bitcast.516, bf16[2048,4096]{1,0:T(8,128)(2,1)} %bitcast.542, bf16[1,896,4096]{2,1,0:T(8,128)(2,1)} %param.20), kind=kOutput, calls=%fused_computation.136 | convolution fusion | flops 15067248640 | bytes 38813696 | tf_op jit(solution)/shard_map/dot_general | solution.py:167
  817.2 8.7 %all-to-all-start.7 = ((f32[16,1,16]{2,1,0:T(1,128)}), f32[16,1,16]{2,1,0:T(1,128)S(1)}, u32[]{:S(2)}, u32[]{:S(2)}) async-start(f32[16,1,16]{2,1,0:T(1,128)} %bitcast.43), calls=%async_computation.9 | async-start | bytes 16384 | tf_op jit(solution)/shard_map/all_to_all | solution.py:179
  825.9 6.8 pad_maximum_fusion
  832.7 18.7 %copy.206 = bf16[1,2048,2,896]{3,2,1,0:T(2,128)(2,1)} copy(bf16[1,2048,2,896]{1,3,2,0:T(8,128)(2,1)} %pad_maximum_fusion) | data formatting | bytes 14680064
  (630 shorter events, 354.8 us)
Async XLA Ops:
  11.9 15.0 %all-to-all-start.1 = ((f32[8,1,4]{2,1,0:T(1,128)}), f32[8,1,4]{2,1,0:T(1,128)S(1)}, u32[]{:S(2)}, u32[]{:S(2)}) async-start(f32[8,1,4]{2,1,0:T(1,128)} %broadcast_in_dim.223), calls=%async_computation.1 | async-start | bytes 8192 | tf_op jit(solution)/shard_map/all_to_all | solution.py:28
  22.1 2.2 copy-start.3
  26.9 8.9 %copy-start.8 = (f32[4,2048]{1,0:T(4,128)S(1)}, f32[4,2048]{1,0:T(4,128)}, u32[]{:S(2)}) copy-start(f32[4,2048]{1,0:T(4,128)} %param.26) | copy-start | bytes 98308
  28.1 21.1 %all-to-all-start.2 = ((f32[8,4,64,128]{3,2,1,0:T(8,128)}), f32[8,4,64,128]{3,2,1,0:T(8,128)}, u32[]{:S(2)}, u32[]{:S(2)}) async-start(f32[8,4,64,128]{3,2,1,0:T(8,128)} %broadcast_in_dim.226), calls=%async_computation.2 | async-start | bytes 2097152 | tf_op jit(solution)/shard_map/all_to_all | solution.py:28
  36.0 33.7 %copy-start.7 = (bf16[512,256]{1,0:T(8,128)(2,1)S(1)}, bf16[512,256]{1,0:T(8,128)(2,1)}, u32[]{:S(2)}) copy-start(bf16[512,256]{1,0:T(8,128)(2,1)} %param.22) | copy-start | bytes 786436
  50.4 19.4 %all-to-all-start.3 = ((f32[8,4,64,128]{3,2,1,0:T(8,128)}), f32[8,4,64,128]{3,2,1,0:T(8,128)S(1)}, u32[]{:S(2)}, u32[]{:S(2)}) async-start(f32[8,4,64,128]{3,2,1,0:T(8,128)} %broadcast_in_dim.230), calls=%async_computation.3 | async-start | bytes 2097152 | tf_op jit(solution)/shard_map/all_to_all | solution.py:28
  69.7 5.9 copy-start
  71.3 324.1 %all-to-all-start.4 = ((bf16[8,512,256]{2,1,0:T(8,128)(2,1)}), bf16[8,512,256]{2,1,0:T(8,128)(2,1)}, u32[]{:S(2)}, u32[]{:S(2)}) async-start(bf16[8,512,256]{2,1,0:T(8,128)(2,1)} %broadcast_in_dim.238), calls=%async_computation.4 | async-start | bytes 4194304 | tf_op jit(solution)/shard_map/all_to_all | solution.py:28
  75.7 374.2 %reduce-scatter.4.cloned.1.call-start = ((), (), s32[]{:S(2)}) async-start(), calls=%async_computation.11 | async-start | bytes 25165824 | tf_op jit(solution)/shard_map/reduce_scatter | solution.py:80
  78.3 117.4 %copy-start.4 = (f32[4,4,64,128]{3,2,1,0:T(8,128)S(1)}, f32[4,4,64,128]{3,2,1,0:T(8,128)}, u32[]{:S(2)}) copy-start(f32[4,4,64,128]{3,2,1,0:T(8,128)} %get-tuple-element.1303) | copy-start | bytes 1572868
  78.3 117.4 %copy-start.5 = (f32[4,4,64,128]{3,2,1,0:T(8,128)S(1)}, f32[4,4,64,128]{3,2,1,0:T(8,128)}, u32[]{:S(2)}) copy-start(f32[4,4,64,128]{3,2,1,0:T(8,128)} %get-tuple-element.1304) | copy-start | bytes 1572868
  78.3 117.6 %copy-start.10 = (f32[4]{0:T(128)S(1)}, f32[4]{0:T(128)}, u32[]{:S(2)}) copy-start(f32[4]{0:T(128)} %slice_reduce_fusion.3) | copy-start | bytes 52
  393.2 1.9 copy-start.12
  419.3 149.5 %reduce-scatter.6.cloned.1.call-start = ((), (), s32[]{:S(2)}) async-start(), calls=%async_computation.12 | async-start | bytes 9437184 | tf_op jit(solution)/shard_map/reduce_scatter | solution.py:81
  449.9 0.7 copy-start.9
  449.9 118.8 %copy-start.6 = (bf16[128,4096]{1,0:T(8,128)(2,1)S(1)}, bf16[128,4096]{1,0:T(8,128)(2,1)}, u32[]{:S(2)}) copy-start(bf16[128,4096]{1,0:T(8,128)(2,1)} %param.21) | copy-start | bytes 3145732
  450.0 328.2 %all-gather.3.cloned.1.call-start = ((), (), s32[]{:S(2)}) async-start(), calls=%async_computation.13 | async-start | bytes 18874368 | tf_op jit(solution)/shard_map/all_gather | solution.py:162
  577.0 32.7 %copy-start.11 = (f32[128,2]{0,1:T(2,128)S(1)}, f32[128,2]{0,1:T(2,128)}, u32[]{:S(2)}) copy-start(f32[128,2]{0,1:T(2,128)} %param.17) | copy-start | bytes 3076
  610.9 23.9 %all-to-all-start = ((bf16[16,1,16]{2,1,0:T(2,128)(2,1)}), bf16[16,1,16]{2,1,0:T(2,128)(2,1)S(1)}, u32[]{:S(2)}, u32[]{:S(2)}) async-start(bf16[16,1,16]{2,1,0:T(2,128)(2,1)} %copy.185), calls=%async_computation | async-start | bytes 16384 | tf_op jit(solution)/shard_map/all_to_all | solution.py:157
  615.5 194.9 %reduce-scatter.8.cloned.1.call-start = ((), (), s32[]{:S(2)}) async-start(), calls=%async_computation.14 | async-start | bytes 2228224 | tf_op jit(solution)/shard_map/reduce_scatter | solution.py:60
  616.0 44.2 %copy-start.1 = (f32[8,256,128]{2,1,0:T(8,128)S(1)}, f32[8,256,128]{2,1,0:T(8,128)}, u32[]{:S(2)}) copy-start(f32[8,256,128]{2,1,0:T(8,128)} %get-tuple-element.751) | copy-start | bytes 3145732
  616.0 44.2 %copy-start.2 = (f32[8,256,128]{2,1,0:T(8,128)S(1)}, f32[8,256,128]{2,1,0:T(8,128)}, u32[]{:S(2)}) copy-start(f32[8,256,128]{2,1,0:T(8,128)} %get-tuple-element.752) | copy-start | bytes 3145732
  807.0 8.3 all-to-all-start.6
  817.2 34.2 %all-to-all-start.7 = ((f32[16,1,16]{2,1,0:T(1,128)}), f32[16,1,16]{2,1,0:T(1,128)S(1)}, u32[]{:S(2)}, u32[]{:S(2)}) async-start(f32[16,1,16]{2,1,0:T(1,128)} %bitcast.43), calls=%async_computation.9 | async-start | bytes 16384 | tf_op jit(solution)/shard_map/all_to_all | solution.py:179
Sparse Core Ops, SparseCore 0:
  419.4 30.5 reduce-scatter.3
  453.7 114.9 reduce-scatter.5
  609.8 168.3 all-gather.2
Sparse Core Ops, SparseCore 1:
  662.6 147.6 reduce-scatter.7
where the time goes:
time: 869 us; the launch traced here: 862 us
  waiting for transfers between devices  291 us (33%)
  local copies, waits for them, and re-layouts  156 us (18%)
  matrix products  153 us (18%)
  other arithmetic  152 us (17%)
  blocking collectives  58 us (7%)
  starting transfers between devices  36 us (4%)
  between operations  15.7 us (2%)
    reduce_scatter x1, waiting for transfers between devices, summed_rows(): return lax.psum_scatter(tiles, chips, scatter_dimension=0, tiled=True)[0]  117 us
    all_gather x1, waiting for transfers between devices, moe_part(): lax.all_gather(arrived[0], 'seq', axis=0, tiled=True)  116 us
    another operation x54, other arithmetic  53.7 us
    unnamed x41, local copies, waits for them, and re-layouts  47.9 us
    dynamic_update_slice x40, other arithmetic, span_scan(): lax.scan(advance, start_state, (x_spans, b_spans, c_spans, g_spans))  43.9 us
    dot_general x24, matrix products, advance(): scores = jnp.dot(c_block, b_block.T)  34.3 us
    all_to_all x1, blocking collectives, moe_part(): lax.all_to_all(outgoing, EXP, split_axis=0, concat_axis=0, tiled=True)  32.7 us
    dot_general x16, matrix products, advance(): within = jnp.einsum('hij,ij,hjp->hip', weights, scores, x_block)  31 us
  transfers between devices with their start and end apart: 11, of which 6 were waited for; matrix products, arithmetic and copies ran while one was open for 48% of the time, Pallas kernels for 0%

commit v1 on v0

--- a/solution.py
+++ b/solution.py
@@ -126,6 +126,18 @@
 
 
 def moe_part(moe_grad, gates, expert_ids, saved_pre, w_down):
+
+    def edit_streams_on_mesh(vector):
+        return jnp.concatenate(
+            lax.all_to_all(
+                jnp.stack(lax.psum(1, axis_name="seq") * [vector], axis=0),
+                axis_name="seq",
+                split_axis=0,
+                concat_axis=0,
+            ),
+            0,
+        )
+
     tokens_here = moe_grad.shape[0]
     expert_count = lax.axis_size(EXP)
     group_count = lax.axis_size("seq")
@@ -159,7 +171,7 @@
         ).astype(outgoing_gates.dtype),
     )
     gathered, arrived_gates = (
-        lax.all_gather(arrived[0], "seq", axis=0, tiled=True),
+        edit_streams_on_mesh(arrived[0]),
         lax.all_gather(arrived[1].astype(jnp.bfloat16), "seq", axis=0, tiled=True).astype(
             jnp.float32
         ),

time: 869 us -> 1010 us (1.16)
  blocking collectives: 58 us -> 279 us
  waiting for transfers between devices: 291 us -> 204 us
    all_gather x1, blocking collectives: 25.3 us -> 247 us  [moe_part(): lax.all_gather(arrived[1].astype(jnp.bfloat16), 'seq', axis=0, tiled=True)]
    all_gather x1 -> x0, waiting for transfers between devices: 116 us -> none  [moe_part(): lax.all_gather(arrived[0], 'seq', axis=0, tiled=True)]
    reduce_scatter x1, waiting for transfers between devices: 0.03 us -> 41 us  [in_one_piece(): lax.psum_scatter(both, axis, scatter_dimension=dim, tiled=True)]
    unnamed x41 -> x37, local copies, waits for them, and re-layouts: 47.9 us -> 47.9 us
  transfers between devices with their start and end apart: 11 -> 11, of which waited for: 6 -> 5; matrix products, arithmetic and copies ran while one was open for 48% -> 42% of each run, Pallas kernels for 0% -> 0%
where the time goes in v1:
time: 1010 us
  blocking collectives  279 us (28%)
  waiting for transfers between devices  204 us (20%)
  local copies, waits for them, and re-layouts  161 us (16%)
  matrix products  153 us (15%)
  other arithmetic  151 us (15%)
  starting transfers between devices  42.9 us (4%)
  between operations  16 us (2%)
    all_gather x1, blocking collectives, moe_part(): lax.all_gather(arrived[1].astype(jnp.bfloat16), 'seq', axis=0, tiled=True)  247 us
    reduce_scatter x1, waiting for transfers between devices, summed_rows(): return lax.psum_scatter(tiles, chips, scatter_dimension=0, tiled=True)[0]  108 us
    another operation x54, other arithmetic  53.7 us
    unnamed x37, local copies, waits for them, and re-layouts  47.9 us
    dynamic_update_slice x40, other arithmetic, span_scan(): lax.scan(advance, start_state, (x_spans, b_spans, c_spans, g_spans))  43.9 us
    reduce_scatter x1, waiting for transfers between devices, in_one_piece(): lax.psum_scatter(both, axis, scatter_dimension=dim, tiled=True)  41 us
    dot_general x24, matrix products, advance(): scores = jnp.dot(c_block, b_block.T)  34.3 us
    all_to_all x1, blocking collectives, moe_part(): lax.all_to_all(outgoing, EXP, split_axis=0, concat_axis=0, tiled=True)  32 us
  transfers between devices with their start and end apart: 11, of which 5 were waited for; matrix products, arithmetic and copies ran while one was open for 42% of the time, Pallas kernels for 0%

profile of v1, /device:TPU:1, one launch (start us, length us, event | category | flops | bytes accessed | tf_op | source)
XLA Modules:
  0.0 1007.7 jit_solution(12892042197924415907)
XLA Ops:
  11.9 5.9 all-to-all-start.1
  28.1 5.1 all-to-all-start.2
  36.0 13.2 %all-to-all-done.2 = f32[8,4,64,128]{3,2,1,0:T(8,128)} async-done(((f32[8,4,64,128]{3,2,1,0:T(8,128)}), f32[8,4,64,128]{3,2,1,0:T(8,128)}, u32[]{:S(2)}, u32[]{:S(2)}) %all-to-all-start.2) | async-done | bytes 1048608 | tf_op jit(solution)/shard_map/all_to_all | solution.py:28
  58.5 11.1 %all-to-all-done.3 = f32[8,4,64,128]{3,2,1,0:T(8,128)S(1)} async-done(((f32[8,4,64,128]{3,2,1,0:T(8,128)}), f32[8,4,64,128]{3,2,1,0:T(8,128)S(1)}, u32[]{:S(2)}, u32[]{:S(2)}) %all-to-all-start.3) | async-done | bytes 1048608 | tf_op jit(solution)/shard_map/all_to_all | solution.py:28
  76.8 117.4 %while.65 = (s32[]{:T(128)}, f32[4,64,128]{2,1,0:T(8,128)S(1)}, f32[8,4,256,256]{3,2,1,0:T(8,128)}, bf16[8,128,256]{1,2,0:T(8,128)(2,1)}, f32[8,256,256]{2,1,0:T...) while((s32[]{:T(128)}, f32[4,64,128]{2,1,0:T(8,128)S(1)}, ...), condition=%wide.region_8.9_spmd.clone.clone.clone, body=%wide.region_5.8_spmd.clone.clone.sunk.clone | while | flops 53022744 | bytes 6271773 | solution.py:107
  198.2 193.4 %while.66 = (s32[]{:T(128)}, f32[4,64,128]{2,1,0:T(8,128)S(1)}, f32[8,4,256,64]{2,3,1,0:T(8,128)}, f32[8,256,128]{2,1,0:T(8,128)}, f32[8,256,128]{2,1,0:T(8,128)...) while((s32[]{:T(128)}, f32[4,64,128]{2,1,0:T(8,128)S(1)}, ...), condition=%wide.region_16.17_spmd.clone.clone.clone, body=%wide.region_9.16_spmd.clone.clone.sunk.clone | while | flops 170925072 | bytes 11393397 | solution.py:107
  212.2 5.0 reduce-window.78
  236.4 5.0 reduce-window.78
  260.6 5.0 reduce-window.78
  394.0 9.7 convolution_convert_fusion
  403.7 14.0 %copy.201 = bf16[2,8,128,4096]{3,2,1,0:T(8,128)(2,1)} copy(bf16[2,8,128,4096]{3,2,0,1:T(8,128)(2,1)} %bitcast.505) | data formatting | bytes 33554432 | tf_op jit(solution)/shard_map/transpose | solution.py:79
  417.8 30.7 %reduce-scatter.4.cloned.1.call-done = bf16[8,128,4096]{2,1,0:T(8,128)(2,1)} async-done(((bf16[16,128,4096]{2,1,0:T(8,128)(2,1)}), bf16[8,128,4096]{2,1,0:T(8,128)(2,1)}) %reduce-scatter.4.cloned.1.call-update) | async-done | bytes 8388624 | tf_op jit(solution)/shard_map/reduce_scatter | solution.py:80
  451.7 7.4 all-to-all-start
  459.1 108.1 %reduce-scatter.6.cloned.1.call-done = bf16[1,128,4096]{2,1,0:T(8,128)(2,1)} async-done(((bf16[8,128,4096]{2,1,0:T(8,128)(2,1)}), bf16[1,128,4096]{2,1,0:T(8,128)(2,1)}) %reduce-scatter.6.cloned.1.call-update) | async-done | bytes 1048592 | tf_op jit(solution)/shard_map/reduce_scatter | solution.py:81
  575.4 32.0 %all_to_all.61 = bf16[16,16,4096]{2,1,0:T(8,128)(2,1)S(1)} all-to-all(bf16[16,16,4096]{2,1,0:T(8,128)(2,1)S(1)} %bitcast.511), channel_id=1, replica_groups=mesh['seq'=8,'exp_0'=2,'exp_1'=4,'exp_2'=2] {'exp_0','exp_1','exp_2'}, dimensions={0} | all-to-all | bytes 4194304 | tf_op jit(solution)/shard_map/all_to_all | solution.py:168
  607.5 5.9 stack.8
  613.4 6.0 all-to-all-start.6
  619.4 18.7 %copy.202 = bf16[1,2048,2,896]{1,3,2,0:T(8,128)(2,1)} copy(bf16[1,2048,2,896]{3,2,1,0:T(2,128)(2,1)} %param.19) | data formatting | bytes 14680064 | tf_op args[2]
  638.4 246.6 %all-gather = bf16[128,1,16]{2,0,1:T(8,128)(2,1)S(1)} all-gather(bf16[16,1,16]{2,0,1:T(8,128)(2,1)S(1)} %copy.186), channel_id=2, replica_groups=mesh['seq'=8,'exp_0'=2,'exp_1'=4,'exp_2'=2] {'seq'}, dimensions={0}, use_global_device_ids=true | all-gather | bytes 4608 | tf_op jit(solution)/shard_map/all_gather | solution.py:175
  887.3 28.0 %fusion.80 = (bf16[1,2048,1,896]{1,3,2,0:T(8,128)(2,1)}, bf16[1,2048,1,896]{1,3,2,0:T(8,128)(2,1)}, f32[2048]{0:T(1024)S(1)}) fusion(f32[2048]{0:T(1024)S(1)} %reshape.596, bf16[2048,2,896]{0,2,1:T(8,128)(2,1)} %bitcast.516, bf16[2048,4096]{1,0:T(8,128)(2,1)} %bitcast.33, bf16[1,896,4096]{2,1,0:T(8,128)(2,1)} %param.20), kind=kOutput, calls=%fused_computation.136 | convolution fusion | flops 15067248640 | bytes 38813696 | tf_op jit(solution)/shard_map/dot_general | solution.py:179
  919.4 41.0 %reduce-scatter.8.cloned.1.call-done = f32[128,256]{1,0:T(8,128)} async-done(((f32[2048,256]{1,0:T(8,128)}), f32[128,256]{1,0:T(8,128)}) %reduce-scatter.8.cloned.1.call-update) | async-done | bytes 131088 | tf_op jit(solution)/shard_map/reduce_scatter | solution.py:60
  963.8 7.0 all-to-all-start.8
  970.8 6.8 pad_maximum_fusion
  977.6 18.7 %copy.206 = bf16[1,2048,2,896]{3,2,1,0:T(2,128)(2,1)} copy(bf16[1,2048,2,896]{1,3,2,0:T(8,128)(2,1)} %pad_maximum_fusion) | data formatting | bytes 14680064
  (626 shorter events, 360.0 us)
Async XLA Ops:
  11.9 15.1 %all-to-all-start.1 = ((f32[8,1,4]{2,1,0:T(1,128)}), f32[8,1,4]{2,1,0:T(1,128)S(1)}, u32[]{:S(2)}, u32[]{:S(2)}) async-start(f32[8,1,4]{2,1,0:T(1,128)} %broadcast_in_dim.223), calls=%async_computation.1 | async-start | bytes 8192 | tf_op jit(solution)/shard_map/all_to_all | solution.py:28
  22.1 2.2 copy-start.2
  27.0 8.8 copy-start.6
  28.1 21.1 %all-to-all-start.2 = ((f32[8,4,64,128]{3,2,1,0:T(8,128)}), f32[8,4,64,128]{3,2,1,0:T(8,128)}, u32[]{:S(2)}, u32[]{:S(2)}) async-start(f32[8,4,64,128]{3,2,1,0:T(8,128)} %broadcast_in_dim.226), calls=%async_computation.2 | async-start | bytes 2097152 | tf_op jit(solution)/shard_map/all_to_all | solution.py:28
  36.0 33.7 %copy-start.5 = (bf16[512,256]{1,0:T(8,128)(2,1)S(1)}, bf16[512,256]{1,0:T(8,128)(2,1)}, u32[]{:S(2)}) copy-start(bf16[512,256]{1,0:T(8,128)(2,1)} %param.22) | copy-start | bytes 786436
  50.3 19.4 %all-to-all-start.3 = ((f32[8,4,64,128]{3,2,1,0:T(8,128)}), f32[8,4,64,128]{3,2,1,0:T(8,128)S(1)}, u32[]{:S(2)}, u32[]{:S(2)}) async-start(f32[8,4,64,128]{3,2,1,0:T(8,128)} %broadcast_in_dim.230), calls=%async_computation.3 | async-start | bytes 2097152 | tf_op jit(solution)/shard_map/all_to_all | solution.py:28
  71.1 322.9 %all-to-all-start.4 = ((bf16[8,512,256]{2,1,0:T(8,128)(2,1)}), bf16[8,512,256]{2,1,0:T(8,128)(2,1)}, u32[]{:S(2)}, u32[]{:S(2)}) async-start(bf16[8,512,256]{2,1,0:T(8,128)(2,1)} %broadcast_in_dim.238), calls=%async_computation.4 | async-start | bytes 4194304 | tf_op jit(solution)/shard_map/all_to_all | solution.py:28
  75.4 373.0 %reduce-scatter.4.cloned.1.call-start = ((), (), s32[]{:S(2)}) async-start(), calls=%async_computation.12 | async-start | bytes 25165824 | tf_op jit(solution)/shard_map/reduce_scatter | solution.py:80
  76.8 117.4 %copy-start.3 = (f32[4,4,64,128]{3,2,1,0:T(8,128)S(1)}, f32[4,4,64,128]{3,2,1,0:T(8,128)}, u32[]{:S(2)}) copy-start(f32[4,4,64,128]{3,2,1,0:T(8,128)} %get-tuple-element.1304) | copy-start | bytes 1572868
  76.8 117.6 %copy-start.8 = (f32[4]{0:T(128)S(1)}, f32[4]{0:T(128)}, u32[]{:S(2)}) copy-start(f32[4]{0:T(128)} %slice_reduce_fusion.3) | copy-start | bytes 52
  391.7 1.9 copy-start.10
  417.7 149.5 %reduce-scatter.6.cloned.1.call-start = ((), (), s32[]{:S(2)}) async-start(), calls=%async_computation.13 | async-start | bytes 9437184 | tf_op jit(solution)/shard_map/reduce_scatter | solution.py:81
  448.5 0.7 copy-start.7
  448.5 1.9 copy-start.9
  448.5 118.8 %copy-start.4 = (bf16[128,4096]{1,0:T(8,128)(2,1)S(1)}, bf16[128,4096]{1,0:T(8,128)(2,1)}, u32[]{:S(2)}) copy-start(bf16[128,4096]{1,0:T(8,128)(2,1)} %param.21) | copy-start | bytes 3145732
  451.7 123.7 %all-to-all-start = ((bf16[16,1,16]{2,1,0:T(2,128)(2,1)}), bf16[16,1,16]{2,1,0:T(2,128)(2,1)S(1)}, u32[]{:S(2)}, u32[]{:S(2)}) async-start(bf16[16,1,16]{2,1,0:T(2,128)(2,1)} %copy.185), calls=%async_computation | async-start | bytes 16384 | tf_op jit(solution)/shard_map/all_to_all | solution.py:169
  613.4 273.9 %all-to-all-start.6 = ((bf16[8,16,16,4096]{3,2,1,0:T(8,128)(2,1)}), bf16[8,16,16,4096]{3,2,1,0:T(8,128)(2,1)}, u32[]{:S(2)}, u32[]{:S(2)}) async-start(bf16[8,16,16,4096]{3,2,1,0:T(8,128)(2,1)} %stack.8), calls=%async_computation.8 | async-start | bytes 33554432 | tf_op jit(solution)/shard_map/all_to_all | solution.py:132
  619.4 265.7 %copy-start = (f32[8,256,128]{2,1,0:T(8,128)S(1)}, f32[8,256,128]{2,1,0:T(8,128)}, u32[]{:S(2)}) copy-start(f32[8,256,128]{2,1,0:T(8,128)} %get-tuple-element.751) | copy-start | bytes 3145732
  619.4 265.7 %copy-start.1 = (f32[8,256,128]{2,1,0:T(8,128)S(1)}, f32[8,256,128]{2,1,0:T(8,128)}, u32[]{:S(2)}) copy-start(f32[8,256,128]{2,1,0:T(8,128)} %get-tuple-element.752) | copy-start | bytes 3145732
  619.4 341.0 %reduce-scatter.8.cloned.1.call-start = ((), (), s32[]{:S(2)}) async-start(), calls=%async_computation.14 | async-start | bytes 2228224 | tf_op jit(solution)/shard_map/reduce_scatter | solution.py:60
  916.1 45.8 %all-to-all-start.7 = ((f32[8,1,256]{2,1,0:T(1,128)}), f32[8,1,256]{2,1,0:T(1,128)S(1)}, u32[]{:S(2)}, u32[]{:S(2)}) async-start(f32[8,1,256]{2,1,0:T(1,128)} %reshape.657), calls=%async_computation.9 | async-start | bytes 16384 | tf_op jit(solution)/shard_map/all_to_all | solution.py:22
  963.8 32.5 %all-to-all-start.8 = ((f32[16,1,16]{2,1,0:T(1,128)}), f32[16,1,16]{2,1,0:T(1,128)S(1)}, u32[]{:S(2)}, u32[]{:S(2)}) async-start(f32[16,1,16]{2,1,0:T(1,128)} %bitcast.43), calls=%async_computation.10 | async-start | bytes 16384 | tf_op jit(solution)/shard_map/all_to_all | solution.py:191
Sparse Core Ops, SparseCore 0:
  417.9 30.5 reduce-scatter.3
  452.3 114.9 reduce-scatter.5
Sparse Core Ops, SparseCore 1:
  886.6 73.7 reduce-scatter.7
